TPU v7x, 32 devices: a whole 2x2x4 slice. The times are simulated.
32 devices in a mesh: ka: 16 (over z, x, core), pa: 2 (over y).
Axes of the slice: x: 2, y: 2, z: 4, core: 2. Of those that a mesh axis runs over, the one named last changes fastest.
Arguments:
- pairs: bfloat16 [64, 64, 2048], P('pa', 'ka'), may hold values from -6 to 6
- eps_val: float32 [64, 64], P('ka'), may hold values from -1.5 to -0.2
- eps_cond: float32 [64, 64], P('ka'), may hold values from 0.2 to 1.5
- orb_val: bfloat16 [64, 64, 12288], P('ka', None, 'pa'), may hold values from -0.625 to 0.625
- orb_cond: bfloat16 [64, 64, 12288], P('ka', None, 'pa'), may hold values from -0.625 to 0.625
- screened: bfloat16 [12288, 12288], P('ka', 'pa'), may hold values from -0.25 to 0.25
Outputs:
- applied: bfloat16 [64, 64, 2048], P('pa', 'ka')
All inputs are finite; a program needn't handle non-finite values.
Results may differ from a plain program's by a relative error of at most 0.0055.
Values may be sent and summed in bfloat16 or wider, within the bound.
A program may use at most 64 MiB of HBM per device.

v0:
```python
import math

import jax
import jax.numpy as jnp
from jax import lax
from jax.sharding import PartitionSpec as P


def body(pairs, eps_val, eps_cond, orb_val, orb_cond, screened):
    val_rows, kpoints, width = pairs.shape
    all_val = orb_val.shape[1]
    conds = orb_cond.shape[1]
    points_dev = orb_val.shape[2]
    vectors = width // conds
    highest = lax.Precision.HIGHEST
    rows_block = lax.all_gather(pairs, "pa", axis=0, tiled=True)
    row_count = rows_block.shape[0]
    group_size = math.gcd(row_count, 8)
    blocks = rows_block.reshape(row_count // group_size, group_size, kpoints, vectors, conds)

    def fold_handle_group(position, accum):
        coeffs = lax.dynamic_index_in_dim(blocks, position, 0, keepdims=False)
        offset = position * group_size
        valence = lax.dynamic_slice_in_dim(orb_val, offset, group_size, 1)
        inner = jnp.einsum("vkbc,kcm->vkbm", coeffs, orb_cond, preferred_element_type=jnp.float32)
        added = jnp.einsum("vkbm,kvm->bm", inner, valence.astype(jnp.float32), precision=highest)
        return accum + added

    partial_points = lax.fori_loop(
        0, row_count // group_size, fold_handle_group, jnp.zeros((vectors, points_dev), jnp.float32)
    )
    points = lax.psum(partial_points, "ka")
    points_bf = points.astype(jnp.bfloat16)
    image_part = lax.dot_general(
        points_bf, screened, (((1,), (1,)), ((), ())), preferred_element_type=jnp.float32
    )
    image_rows = lax.psum(image_part.astype(jnp.bfloat16), "pa")
    image_whole = lax.all_gather(image_rows, "ka", axis=1, tiled=True)
    image_block = lax.dynamic_slice_in_dim(
        image_whole, lax.axis_index("pa") * points_dev, points_dev, 1
    )
    image_wide = image_block.astype(jnp.float32)
    back_group_size = math.gcd(all_val, 8)

    def back_handle_group(position):
        offset = position * back_group_size
        valence = lax.dynamic_slice_in_dim(orb_val, offset, back_group_size, 1)
        weighted = (valence.astype(jnp.float32)[:, :, None, :] * image_wide[None, None]).astype(
            jnp.bfloat16
        )
        coupling = jnp.einsum(
            "kvbm,kcm->vkbc", weighted, orb_cond, preferred_element_type=jnp.float32
        )
        return coupling.reshape(back_group_size, kpoints, vectors * conds)

    results = lax.map(back_handle_group, jnp.arange(all_val // back_group_size, dtype=jnp.int32))
    summed_all = lax.psum(
        results.reshape(all_val, kpoints, vectors * conds).astype(jnp.bfloat16), "pa"
    ).astype(jnp.float32)
    coupling = lax.dynamic_slice_in_dim(summed_all, lax.axis_index("pa") * val_rows, val_rows, 0)
    own_val = lax.dynamic_slice_in_dim(eps_val, lax.axis_index("pa") * val_rows, val_rows, 1)
    energy_gap = eps_cond[None, :, None, :] - jnp.transpose(own_val)[:, :, None, None]
    coeffs = pairs.astype(jnp.float32).reshape(val_rows, kpoints, vectors, conds)
    diagonal_part = (energy_gap * coeffs).reshape(val_rows, kpoints, vectors * conds)
    return (diagonal_part + coupling).astype(jnp.bfloat16)


def solution(mesh):
    in_specs = (
        P("pa", "ka", None),
        P("ka", None),
        P("ka", None),
        P("ka", None, "pa"),
        P("ka", None, "pa"),
        P("ka", "pa"),
    )
    out_specs = P("pa", "ka", None)
    return jax.shard_map(body, mesh=mesh, in_specs=in_specs, out_specs=out_specs, check_vma=False)
```

profile of v0, /device:TPU:0, one launch (start us, length us, event | category | flops | bytes accessed | tf_op | source)
XLA Modules:
  0.0 309.9 jit_solution(8324621128068602403)
XLA Ops:
  6.5 0.7 all-gather.2.cloned.1.call-update
  7.3 25.6 %all-gather.2.cloned.1.call-done = bf16[64,4,2048]{2,1,0:T(4,128)(2,1)} async-done(((bf16[32,4,2048]{2,1,0:T(4,128)(2,1)}), bf16[64,4,2048]{2,1,0:T(4,128)(2,1)}) %all-gather.2.cloned.1.call-update) | async-done | bytes 1048592 | tf_op jit(solution)/shard_map/all_gather | solution.py:16
  32.9 3.4 %reshape.23 = bf16[8,8,4,32,64]{4,3,2,1,0:T(8,128)(2,1)S(1)} reshape(bf16[64,4,2048]{2,1,0:T(4,128)(2,1)} %all-gather.2.cloned.1.call-done) | data formatting | bytes 2097152 | tf_op jit(solution)/shard_map/reshape | solution.py:19
  36.3 55.7 %while.25 = (s32[]{:T(128)}, f32[32,6144]{1,0:T(8,128)S(1)}, bf16[4,64,6144]{2,1,0:T(8,128)(2,1)}, bf16[8,8,4,32,64]{4,3,2,1,0:T(8,128)(2,1)S(1)}, bf16[4,64,614...) while((s32[]{:T(128)}, f32[32,6144]{1,0:T(8,128)S(1)}, ...), condition=%wide.region_1.2_spmd.clone, body=%wide.region_0.1_spmd.clone.sunk | while | flops 818282496 | bytes 8519845 | solution.py:29
  36.3 1.1 bitcast_convert_fusion.2
  37.4 5.6 %fusion.22 = f32[6144,32]{0,1:T(8,128)S(1)} fusion(f32[6144,4,8]{0,2,1:T(8,128)S(1)} %bitcast_convert_fusion.2, bf16[4,64,6144]{2,1,0:T(8,128)(2,1)} %get-tuple-element.263, bf16[8,8,4,32,64]{4,3,2,1,0:T(8,128)(2,1)S(1)} %get-tuple-element.262, s32[]{:T(128)S(6)} %copy.29), kind=kOutput, calls=%fused_computation.9.clone.1 | convolution fusion | flops 817692672 | bytes 4980740 | tf_op jit(solution)/shard_map/while/body/eval_jaxpr/vkbc,kcm->vkbm/dot_general | solution.py:25
  43.0 0.2 bitcast_add_fusion.2
  43.3 1.1 bitcast_convert_fusion.2
  44.4 5.6 %fusion.22 = f32[6144,32]{0,1:T(8,128)S(1)} fusion(f32[6144,4,8]{0,2,1:T(8,128)S(1)} %bitcast_convert_fusion.2, bf16[4,64,6144]{2,1,0:T(8,128)(2,1)} %get-tuple-element.263, bf16[8,8,4,32,64]{4,3,2,1,0:T(8,128)(2,1)S(1)} %get-tuple-element.262, s32[]{:T(128)S(6)} %copy.29), kind=kOutput, calls=%fused_computation.9.clone.1 | convolution fusion | flops 817692672 | bytes 4980740 | tf_op jit(solution)/shard_map/while/body/eval_jaxpr/vkbc,kcm->vkbm/dot_general | solution.py:25
  50.0 0.2 bitcast_add_fusion.2
  50.3 1.1 bitcast_convert_fusion.2
  51.3 5.6 %fusion.22 = f32[6144,32]{0,1:T(8,128)S(1)} fusion(f32[6144,4,8]{0,2,1:T(8,128)S(1)} %bitcast_convert_fusion.2, bf16[4,64,6144]{2,1,0:T(8,128)(2,1)} %get-tuple-element.263, bf16[8,8,4,32,64]{4,3,2,1,0:T(8,128)(2,1)S(1)} %get-tuple-element.262, s32[]{:T(128)S(6)} %copy.29), kind=kOutput, calls=%fused_computation.9.clone.1 | convolution fusion | flops 817692672 | bytes 4980740 | tf_op jit(solution)/shard_map/while/body/eval_jaxpr/vkbc,kcm->vkbm/dot_general | solution.py:25
  57.0 0.2 bitcast_add_fusion.2
  57.2 1.1 bitcast_convert_fusion.2
  58.3 5.6 %fusion.22 = f32[6144,32]{0,1:T(8,128)S(1)} fusion(f32[6144,4,8]{0,2,1:T(8,128)S(1)} %bitcast_convert_fusion.2, bf16[4,64,6144]{2,1,0:T(8,128)(2,1)} %get-tuple-element.263, bf16[8,8,4,32,64]{4,3,2,1,0:T(8,128)(2,1)S(1)} %get-tuple-element.262, s32[]{:T(128)S(6)} %copy.29), kind=kOutput, calls=%fused_computation.9.clone.1 | convolution fusion | flops 817692672 | bytes 4980740 | tf_op jit(solution)/shard_map/while/body/eval_jaxpr/vkbc,kcm->vkbm/dot_general | solution.py:25
  64.2 1.1 bitcast_convert_fusion.2
  65.3 5.6 %fusion.22 = f32[6144,32]{0,1:T(8,128)S(1)} fusion(f32[6144,4,8]{0,2,1:T(8,128)S(1)} %bitcast_convert_fusion.2, bf16[4,64,6144]{2,1,0:T(8,128)(2,1)} %get-tuple-element.263, bf16[8,8,4,32,64]{4,3,2,1,0:T(8,128)(2,1)S(1)} %get-tuple-element.262, s32[]{:T(128)S(6)} %copy.29), kind=kOutput, calls=%fused_computation.9.clone.1 | convolution fusion | flops 817692672 | bytes 4980740 | tf_op jit(solution)/shard_map/while/body/eval_jaxpr/vkbc,kcm->vkbm/dot_general | solution.py:25
  71.2 1.1 bitcast_convert_fusion.2
  72.2 5.6 %fusion.22 = f32[6144,32]{0,1:T(8,128)S(1)} fusion(f32[6144,4,8]{0,2,1:T(8,128)S(1)} %bitcast_convert_fusion.2, bf16[4,64,6144]{2,1,0:T(8,128)(2,1)} %get-tuple-element.263, bf16[8,8,4,32,64]{4,3,2,1,0:T(8,128)(2,1)S(1)} %get-tuple-element.262, s32[]{:T(128)S(6)} %copy.29), kind=kOutput, calls=%fused_computation.9.clone.1 | convolution fusion | flops 817692672 | bytes 4980740 | tf_op jit(solution)/shard_map/while/body/eval_jaxpr/vkbc,kcm->vkbm/dot_general | solution.py:25
  78.1 1.1 bitcast_convert_fusion.2
  79.2 5.6 %fusion.22 = f32[6144,32]{0,1:T(8,128)S(1)} fusion(f32[6144,4,8]{0,2,1:T(8,128)S(1)} %bitcast_convert_fusion.2, bf16[4,64,6144]{2,1,0:T(8,128)(2,1)} %get-tuple-element.263, bf16[8,8,4,32,64]{4,3,2,1,0:T(8,128)(2,1)S(1)} %get-tuple-element.262, s32[]{:T(128)S(6)} %copy.29), kind=kOutput, calls=%fused_computation.9.clone.1 | convolution fusion | flops 817692672 | bytes 4980740 | tf_op jit(solution)/shard_map/while/body/eval_jaxpr/vkbc,kcm->vkbm/dot_general | solution.py:25
  85.1 1.1 bitcast_convert_fusion.2
  86.1 5.6 %fusion.22 = f32[6144,32]{0,1:T(8,128)S(1)} fusion(f32[6144,4,8]{0,2,1:T(8,128)S(1)} %bitcast_convert_fusion.2, bf16[4,64,6144]{2,1,0:T(8,128)(2,1)} %get-tuple-element.263, bf16[8,8,4,32,64]{4,3,2,1,0:T(8,128)(2,1)S(1)} %get-tuple-element.262, s32[]{:T(128)S(6)} %copy.29), kind=kOutput, calls=%fused_computation.9.clone.1 | convolution fusion | flops 817692672 | bytes 4980740 | tf_op jit(solution)/shard_map/while/body/eval_jaxpr/vkbc,kcm->vkbm/dot_general | solution.py:25
  92.0 69.3 %all-reduce.4 = bf16[32,6144]{1,0:T(8,128)(2,1)S(1)} all-reduce(f32[32,6144]{1,0:T(8,128)S(1)} %get-tuple-element.131), channel_id=1, replica_groups=mesh['ka'=16,'pa'=2] {'ka'}, use_global_device_ids=true, to_apply=%region_2.3 | all-reduce | flops 196608 | bytes 1179648 | tf_op jit(solution)/shard_map/psum | solution.py:32
  161.4 6.7 %convolution_convert_fusion = bf16[32,768]{1,0:T(8,128)(2,1)S(1)} fusion(bf16[768,6144]{1,0:T(8,128)(2,1)} %param.15, bf16[32,6144]{1,0:T(8,128)(2,1)S(1)} %all-reduce.4), kind=kOutput, calls=%fused_computation.15 | convolution fusion | flops 302014464 | bytes 9879552 | tf_op jit(solution)/shard_map/dot_general | solution.py:34
  168.1 7.7 %psum.22 = bf16[32,768]{1,0:T(8,128)(2,1)S(1)} all-reduce(bf16[32,768]{1,0:T(8,128)(2,1)S(1)} %convolution_convert_fusion), channel_id=1, replica_groups=mesh['ka'=16,'pa'=2] {'pa'}, use_global_device_ids=true, to_apply=%region_3.4 | all-reduce | flops 24576 | bytes 98304 | tf_op jit(solution)/shard_map/psum | solution.py:37
  175.7 19.8 %all_gather.7 = bf16[32,12288]{1,0:T(8,128)(2,1)S(1)} all-gather(bf16[32,768]{1,0:T(8,128)(2,1)S(1)} %psum.22), channel_id=1, replica_groups=mesh['ka'=16,'pa'=2] {'ka'}, dimensions={1}, use_global_device_ids=true | all-gather | bytes 835584 | tf_op jit(solution)/shard_map/all_gather | solution.py:38
  195.6 64.3 %while.24 = (s32[]{:T(128)}, bf16[8,8,4,2048]{3,1,2,0:T(8,128)(2,1)S(1)}, s32[8]{0:T(128)S(1)}, bf16[4,64,6144]{2,1,0:T(8,128)(2,1)}, f32[32,6144]{1,0:T(8,128)S...) while((s32[]{:T(128)}, bf16[8,8,4,2048]{3,1,2,0:T(8,128)(2,1)S(1)}, ...), condition=%wide.region_5.6_spmd, body=%wide.region_4.5_spmd.sunk | while | flops 818085888 | bytes 6553775 | solution.py:56
  195.6 0.7 dynamic_slice.50
  197.0 1.1 dynamic-slice_convert_fusion.3
  198.0 5.3 %fusion.19 = bf16[8,4,32,64]{3,2,0,1:T(8,128)(2,1)S(1)} fusion(bf16[4,64,6144]{2,1,0:T(8,128)(2,1)} %get-tuple-element.293, f32[32,6144]{1,0:T(8,128)S(1)} %get-tuple-element.292, f32[4,8,6144]{2,1,0:T(8,128)S(1)} %dynamic-slice_convert_fusion.3), kind=kOutput, calls=%fused_computation.5.clone.1 | convolution fusion | flops 817889280 | bytes 4849664 | tf_op jit(solution)/shard_map/while/body/eval_jaxpr/kvbm,kcm->vkbc/dot_general | solution.py:51
  203.3 0.3 broadcast_in_dim.17
  203.7 0.7 dynamic_slice.50
  205.0 1.1 dynamic-slice_convert_fusion.3
  206.1 5.3 %fusion.19 = bf16[8,4,32,64]{3,2,0,1:T(8,128)(2,1)S(1)} fusion(bf16[4,64,6144]{2,1,0:T(8,128)(2,1)} %get-tuple-element.293, f32[32,6144]{1,0:T(8,128)S(1)} %get-tuple-element.292, f32[4,8,6144]{2,1,0:T(8,128)S(1)} %dynamic-slice_convert_fusion.3), kind=kOutput, calls=%fused_computation.5.clone.1 | convolution fusion | flops 817889280 | bytes 4849664 | tf_op jit(solution)/shard_map/while/body/eval_jaxpr/kvbm,kcm->vkbc/dot_general | solution.py:51
  211.4 0.3 broadcast_in_dim.17
  211.7 0.7 dynamic_slice.50
  213.1 1.1 dynamic-slice_convert_fusion.3
  214.1 5.3 %fusion.19 = bf16[8,4,32,64]{3,2,0,1:T(8,128)(2,1)S(1)} fusion(bf16[4,64,6144]{2,1,0:T(8,128)(2,1)} %get-tuple-element.293, f32[32,6144]{1,0:T(8,128)S(1)} %get-tuple-element.292, f32[4,8,6144]{2,1,0:T(8,128)S(1)} %dynamic-slice_convert_fusion.3), kind=kOutput, calls=%fused_computation.5.clone.1 | convolution fusion | flops 817889280 | bytes 4849664 | tf_op jit(solution)/shard_map/while/body/eval_jaxpr/kvbm,kcm->vkbc/dot_general | solution.py:51
  219.4 0.3 broadcast_in_dim.17
  219.7 0.7 dynamic_slice.50
  221.1 1.1 dynamic-slice_convert_fusion.3
  222.2 5.3 %fusion.19 = bf16[8,4,32,64]{3,2,0,1:T(8,128)(2,1)S(1)} fusion(bf16[4,64,6144]{2,1,0:T(8,128)(2,1)} %get-tuple-element.293, f32[32,6144]{1,0:T(8,128)S(1)} %get-tuple-element.292, f32[4,8,6144]{2,1,0:T(8,128)S(1)} %dynamic-slice_convert_fusion.3), kind=kOutput, calls=%fused_computation.5.clone.1 | convolution fusion | flops 817889280 | bytes 4849664 | tf_op jit(solution)/shard_map/while/body/eval_jaxpr/kvbm,kcm->vkbc/dot_general | solution.py:51
  227.5 0.3 broadcast_in_dim.17
  227.8 0.7 dynamic_slice.50
  229.1 1.1 dynamic-slice_convert_fusion.3
  230.2 5.3 %fusion.19 = bf16[8,4,32,64]{3,2,0,1:T(8,128)(2,1)S(1)} fusion(bf16[4,64,6144]{2,1,0:T(8,128)(2,1)} %get-tuple-element.293, f32[32,6144]{1,0:T(8,128)S(1)} %get-tuple-element.292, f32[4,8,6144]{2,1,0:T(8,128)S(1)} %dynamic-slice_convert_fusion.3), kind=kOutput, calls=%fused_computation.5.clone.1 | convolution fusion | flops 817889280 | bytes 4849664 | tf_op jit(solution)/shard_map/while/body/eval_jaxpr/kvbm,kcm->vkbc/dot_general | solution.py:51
  235.5 0.3 broadcast_in_dim.17
  235.8 0.7 dynamic_slice.50
  237.2 1.1 dynamic-slice_convert_fusion.3
  238.2 5.3 %fusion.19 = bf16[8,4,32,64]{3,2,0,1:T(8,128)(2,1)S(1)} fusion(bf16[4,64,6144]{2,1,0:T(8,128)(2,1)} %get-tuple-element.293, f32[32,6144]{1,0:T(8,128)S(1)} %get-tuple-element.292, f32[4,8,6144]{2,1,0:T(8,128)S(1)} %dynamic-slice_convert_fusion.3), kind=kOutput, calls=%fused_computation.5.clone.1 | convolution fusion | flops 817889280 | bytes 4849664 | tf_op jit(solution)/shard_map/while/body/eval_jaxpr/kvbm,kcm->vkbc/dot_general | solution.py:51
  243.5 0.3 broadcast_in_dim.17
  243.8 0.7 dynamic_slice.50
  245.2 1.1 dynamic-slice_convert_fusion.3
  246.3 5.3 %fusion.19 = bf16[8,4,32,64]{3,2,0,1:T(8,128)(2,1)S(1)} fusion(bf16[4,64,6144]{2,1,0:T(8,128)(2,1)} %get-tuple-element.293, f32[32,6144]{1,0:T(8,128)S(1)} %get-tuple-element.292, f32[4,8,6144]{2,1,0:T(8,128)S(1)} %dynamic-slice_convert_fusion.3), kind=kOutput, calls=%fused_computation.5.clone.1 | convolution fusion | flops 817889280 | bytes 4849664 | tf_op jit(solution)/shard_map/while/body/eval_jaxpr/kvbm,kcm->vkbc/dot_general | solution.py:51
  251.6 0.3 broadcast_in_dim.17
  251.9 0.7 dynamic_slice.50
  253.2 1.1 dynamic-slice_convert_fusion.3
  254.3 5.3 %fusion.19 = bf16[8,4,32,64]{3,2,0,1:T(8,128)(2,1)S(1)} fusion(bf16[4,64,6144]{2,1,0:T(8,128)(2,1)} %get-tuple-element.293, f32[32,6144]{1,0:T(8,128)S(1)} %get-tuple-element.292, f32[4,8,6144]{2,1,0:T(8,128)S(1)} %dynamic-slice_convert_fusion.3), kind=kOutput, calls=%fused_computation.5.clone.1 | convolution fusion | flops 817889280 | bytes 4849664 | tf_op jit(solution)/shard_map/while/body/eval_jaxpr/kvbm,kcm->vkbc/dot_general | solution.py:51
  259.6 0.3 broadcast_in_dim.17
  259.9 1.9 copy.10
  262.2 0.8 mul.46
  263.1 37.5 %all-reduce.3.cloned.1.call-done = bf16[64,4,2048]{2,1,0:T(4,128)(2,1)} async-done(((bf16[64,4,2048]{2,1,0:T(4,128)(2,1)}), bf16[64,4,2048]{2,1,0:T(4,128)(2,1)}) %all-reduce.3.cloned.1.call-update) | async-done | bytes 1048592 | tf_op jit(solution)/shard_map/psum | solution.py:57
  300.6 2.5 add_convert_fusion
  (30 shorter events, 1.8 us)
Async XLA Ops:
  6.5 255.3 %copy-start = (f32[4,64]{1,0:T(4,128)S(1)}, f32[4,64]{1,0:T(4,128)}, u32[]{:S(2)}) copy-start(f32[4,64]{1,0:T(4,128)} %param.11) | copy-start | bytes 3076
  6.5 26.4 %all-gather.2.cloned.1.call-start = ((), (), s32[]{:S(2)}) async-start(), calls=%async_computation | async-start | bytes 1572864 | tf_op jit(solution)/shard_map/all_gather | solution.py:16
  7.3 293.3 %all-reduce.3.cloned.1.call-start = ((), (), s32[]{:S(2)}) async-start(), calls=%async_computation.1 | async-start | bytes 2097152 | tf_op jit(solution)/shard_map/psum | solution.py:57
  161.4 34.2 %copy-start.1 = (bf16[8,8,4,2048]{3,1,2,0:T(8,128)(2,1)S(1)}, bf16[8,8,4,2048]{3,1,2,0:T(8,128)(2,1)}, u32[]{:S(2)}) copy-start(bf16[8,8,4,2048]{3,1,2,0:T(8,128)(2,1)} %custom-call.1) | copy-start | bytes 3145732
  259.9 2.1 copy-start.2
Sparse Core Ops, SparseCore 0:
  8.9 23.9 all-gather.1
  261.9 38.5 all-reduce.2
where the time goes:
time: 311 us; the launch traced here: 310 us
  blocking collectives  96.8 us (31%)
  matrix products  94.2 us (30%)
  waiting for transfers between devices  63.8 us (21%)
  other arithmetic  21.3 us (7%)
  local copies, waits for them, and re-layouts  14.1 us (5%)
  between operations  13.5 us (4%)
  loops' own time  6.19 us (2%)
    psum x1, blocking collectives, body(): points = lax.psum(partial_points, 'ka')  69.3 us
    dot_general x8, matrix products, fold_handle_group(): jnp.einsum('vkbc,kcm->vkbm', coeffs, orb_cond, preferred_element_type=jnp...  45.1 us
    dot_general x8, matrix products, back_handle_group(): jnp.einsum('kvbm,kcm->vkbc', weighted, orb_cond, preferred_element_type=j...  42.4 us
    psum x1, waiting for transfers between devices, body(): lax.psum(results.reshape(all_val, kpoints, vectors * conds).astype(jnp.bf...  37.5 us
    all_gather x1, waiting for transfers between devices, body(): rows_block = lax.all_gather(pairs, 'pa', axis=0, tiled=True)  25.6 us
    all_gather x1, blocking collectives, body(): image_whole = lax.all_gather(image_rows, 'ka', axis=1, tiled=True)  19.8 us
    convert_element_type x8, other arithmetic, back_handle_group(): valence.astype(jnp.float32)[:, :, None, :] * image_wide[None, None]  8.43 us
    while x8, other arithmetic  8.43 us
  transfers between devices with their start and end apart: 2, of which 2 were waited for; matrix products, arithmetic and copies ran while one was open for 0% of the time, Pallas kernels for 0%

commit v1 on v0

v1 whole, which is shorter than its diff:
```python
import functools

import jax
import jax.numpy as jnp
from jax import lax
from jax.experimental import pallas as pl
from jax.experimental.pallas import tpu as pltpu
from jax.sharding import PartitionSpec as P

VMEM_BYTES = 58 * 1024 * 1024


def pick_tile(extent, most):
    tile = most
    while extent % tile:
        tile //= 2
    return tile


def forward_kernel(vectors, pairs_ref, val_ref, cond_ref, out_ref, turned):
    kpoints, conds = cond_ref.shape[0], cond_ref.shape[1]
    tile = cond_ref.shape[2]

    @pl.when(pl.program_id(0) == 0)
    def _():
        for k in range(kpoints):
            turned[k] = pairs_ref[k].T

    group = 4
    wide = [cond_ref[k].astype(jnp.float32).reshape(conds // 8, 8, tile) for k in range(kpoints)]
    for g in range(vectors // group):
        total = None
        for k in range(kpoints):
            rows = turned[k, g * group * conds : (g + 1) * group * conds, :]
            inner = jnp.dot(rows, val_ref[k], preferred_element_type=jnp.float32)
            inner = inner.reshape(group, conds // 8, 8, tile)
            added = jnp.sum(inner * wide[k][None], axis=1)
            total = added if total is None else total + added
        out_ref[g * group : (g + 1) * group, :] = jnp.sum(total, axis=1)


def forward(rows, orb_val, orb_cond):
    kpoints, all_val, points_dev = orb_val.shape
    conds = orb_cond.shape[1]
    width = rows.shape[2]
    vectors = width // conds
    tile = pick_tile(points_dev, 256)
    return pl.pallas_call(
        functools.partial(forward_kernel, vectors),
        grid=(points_dev // tile,),
        out_shape=jax.ShapeDtypeStruct((vectors, points_dev), jnp.float32),
        in_specs=[
            pl.BlockSpec((kpoints, all_val, width), lambda i: (0, 0, 0)),
            pl.BlockSpec((kpoints, all_val, tile), lambda i: (0, 0, i)),
            pl.BlockSpec((kpoints, conds, tile), lambda i: (0, 0, i)),
        ],
        out_specs=pl.BlockSpec((vectors, tile), lambda i: (0, i)),
        scratch_shapes=[pltpu.VMEM((kpoints, width, all_val), jnp.bfloat16)],
        compiler_params=pltpu.CompilerParams(vmem_limit_bytes=VMEM_BYTES),
    )(rows, orb_val, orb_cond)


def backward_kernel(image_ref, val_ref, cond_ref, out_ref, total):
    vectors, tile = image_ref.shape
    conds = cond_ref.shape[1]
    group = 4
    step = pl.program_id(1)

    @pl.when(step == 0)
    def _():
        total[...] = jnp.zeros_like(total)

    valence = val_ref[0]
    conduction = cond_ref[0]
    for g in range(vectors // group):
        pieces = [
            jnp.broadcast_to(image_ref[b : b + 1, :], (conds, tile)) * conduction
            for b in range(g * group, (g + 1) * group)
        ]
        mixed = jnp.concatenate(pieces, axis=0)
        cols = slice(g * group * conds, (g + 1) * group * conds)
        total[:, cols] += lax.dot_general(
            valence, mixed, (((1,), (1,)), ((), ())), preferred_element_type=jnp.float32
        )

    @pl.when(step == pl.num_programs(1) - 1)
    def _():
        out_ref[0] = total[...].astype(out_ref.dtype)


def backward(image, orb_val, orb_cond):
    kpoints, all_val, points_dev = orb_val.shape
    conds = orb_cond.shape[1]
    vectors = image.shape[0]
    tile = pick_tile(points_dev, 1024)
    return pl.pallas_call(
        backward_kernel,
        grid=(kpoints, points_dev // tile),
        out_shape=jax.ShapeDtypeStruct((kpoints, all_val, vectors * conds), jnp.bfloat16),
        in_specs=[
            pl.BlockSpec((vectors, tile), lambda k, i: (0, i)),
            pl.BlockSpec((1, all_val, tile), lambda k, i: (k, 0, i)),
            pl.BlockSpec((1, conds, tile), lambda k, i: (k, 0, i)),
        ],
        out_specs=pl.BlockSpec((1, all_val, vectors * conds), lambda k, i: (k, 0, 0)),
        scratch_shapes=[pltpu.VMEM((all_val, vectors * conds), jnp.float32)],
        compiler_params=pltpu.CompilerParams(vmem_limit_bytes=VMEM_BYTES),
    )(image, orb_val, orb_cond)


def body(pairs, eps_val, eps_cond, orb_val, orb_cond, screened):
    val_rows, kpoints, width = pairs.shape
    conds = orb_cond.shape[1]
    points_dev = orb_val.shape[2]
    vectors = width // conds
    own = jnp.transpose(pairs, (1, 0, 2))
    rows = lax.all_gather(own, "pa", axis=1, tiled=True)
    partial_points = forward(rows, orb_val, orb_cond)
    points = lax.psum_scatter(partial_points, "ka", scatter_dimension=1, tiled=True)
    points_bf = lax.all_gather(points.astype(jnp.bfloat16), "ka", axis=1, tiled=True)
    image_part = lax.dot_general(
        points_bf, screened, (((1,), (1,)), ((), ())), preferred_element_type=jnp.float32
    )
    image_rows = lax.psum(image_part.astype(jnp.bfloat16), "pa")
    image_whole = lax.all_gather(image_rows, "ka", axis=1, tiled=True)
    image_block = lax.dynamic_slice_in_dim(
        image_whole, lax.axis_index("pa") * points_dev, points_dev, 1
    )
    results = backward(image_block, orb_val, orb_cond)
    coupling = lax.psum_scatter(results, "pa", scatter_dimension=1, tiled=True)
    coupling = jnp.transpose(coupling.astype(jnp.float32), (1, 0, 2))
    own_val = lax.dynamic_slice_in_dim(eps_val, lax.axis_index("pa") * val_rows, val_rows, 1)
    energy_gap = eps_cond[None, :, None, :] - jnp.transpose(own_val)[:, :, None, None]
    coeffs = pairs.astype(jnp.float32).reshape(val_rows, kpoints, vectors, conds)
    diagonal_part = (energy_gap * coeffs).reshape(val_rows, kpoints, vectors * conds)
    return (diagonal_part + coupling).astype(jnp.bfloat16)


def solution(mesh):
    in_specs = (
        P("pa", "ka", None),
        P("ka", None),
        P("ka", None),
        P("ka", None, "pa"),
        P("ka", None, "pa"),
        P("ka", "pa"),
    )
    out_specs = P("pa", "ka", None)
    return jax.shard_map(body, mesh=mesh, in_specs=in_specs, out_specs=out_specs, check_vma=False)
```

time: 311 us -> 244 us (0.78)
  matrix products: 94.2 us -> 6.59 us
  Pallas kernels: 0 us -> 69 us
  blocking collectives: 96.8 us -> 48.7 us
  waiting for transfers between devices: 63.8 us -> 98.2 us
  other arithmetic: 21.3 us -> 2.49 us
  local copies, waits for them, and re-layouts: 14.1 us -> 4.98 us
  loops' own time: 6.19 us -> 0 us
    dot_general x16 -> x0, matrix products: 87.5 us -> none  [the longest x8 45.1 us: fold_handle_group(): jnp.einsum('vkbc,kcm->vkbm', coeffs, orb_cond, preferred_element_type=jnp...]
    reduce_scatter x0 -> x2, waiting for transfers between devices: none -> 74 us  [the longest x1 56.8 us: body(): lax.psum_scatter(partial_points, 'ka', scatter_dimension=1, tiled=True)]
    psum x1 -> x0, blocking collectives: 69.3 us -> none  [body(): points = lax.psum(partial_points, 'ka')]
    pallas_call x0 -> x2, Pallas kernels: none -> 69 us  [the longest x1 36.1 us: backward(): pl.pallas_call(backward_kernel, grid=(kpoints, points_dev // tile), out_s...]
    psum x1 -> x0, waiting for transfers between devices: 37.5 us -> none  [body(): lax.psum(results.reshape(all_val, kpoints, vectors * conds).astype(jnp.bf...]
    all_gather x0 -> x1, blocking collectives: none -> 20.5 us  [body(): lax.all_gather(points.astype(jnp.bfloat16), 'ka', axis=1, tiled=True)]
    while x8 -> x0, other arithmetic: 8.43 us -> none
    convert_element_type x9 -> x1, other arithmetic: 8.48 us -> 0.8 us  [body(): points.astype(jnp.bfloat16)]
  transfers between devices with their start and end apart: 2 -> 3, of which waited for: 2 -> 3; matrix products, arithmetic and copies ran while one was open for 0% -> 0% of each run, Pallas kernels for 0% -> 0%
where the time goes in v1:
time: 244 us; the launch traced here: 243 us
  waiting for transfers between devices  98.2 us (40%)
  Pallas kernels  69 us (28%)
  blocking collectives  48.7 us (20%)
  between operations  13.2 us (5%)
  matrix products  6.59 us (3%)
  local copies, waits for them, and re-layouts  4.98 us (2%)
  other arithmetic  2.49 us (1%)
    reduce_scatter x1, waiting for transfers between devices, body(): lax.psum_scatter(partial_points, 'ka', scatter_dimension=1, tiled=True)  56.8 us
    pallas_call x1, Pallas kernels, backward(): pl.pallas_call(backward_kernel, grid=(kpoints, points_dev // tile), out_s...  36.1 us
    pallas_call x1, Pallas kernels, forward(): pl.pallas_call(functools.partial(forward_kernel, vectors), grid=(points_d...  32.9 us
    all_gather x1, waiting for transfers between devices, body(): rows = lax.all_gather(own, 'pa', axis=1, tiled=True)  24.2 us
    all_gather x1, blocking collectives, body(): lax.all_gather(points.astype(jnp.bfloat16), 'ka', axis=1, tiled=True)  20.5 us
    all_gather x1, blocking collectives, body(): image_whole = lax.all_gather(image_rows, 'ka', axis=1, tiled=True)  19.6 us
    reduce_scatter x1, waiting for transfers between devices, body(): coupling = lax.psum_scatter(results, 'pa', scatter_dimension=1, tiled=True)  17.1 us
    psum x1, blocking collectives, body(): image_rows = lax.psum(image_part.astype(jnp.bfloat16), 'pa')  8.61 us
  transfers between devices with their start and end apart: 3, of which 3 were waited for; matrix products, arithmetic and copies ran while one was open for 0% of the time, Pallas kernels for 0%

profile of v1, /device:TPU:0, one launch (start us, length us, event | category | flops | bytes accessed | tf_op | source)
XLA Modules:
  0.0 243.2 jit_solution(10783406591022124009)
XLA Ops:
  6.5 0.0 copy-start
  6.5 0.0 all-gather.2.cloned.1.call-start
  6.5 2.1 copy.12
  8.7 0.0 all-gather.2.cloned.1.call-update
  8.7 0.0 reduce-scatter.3.cloned.1.call-start
  8.8 24.2 %all-gather.2.cloned.1.call-done.pairs_ref = bf16[4,64,2048]{2,1,0:T(8,128)(2,1)} async-done(((bf16[4,32,2048]{2,1,0:T(8,128)(2,1)}), bf16[4,64,2048]{2,1,0:T(8,128)(2,1)}) %all-gather.2.cloned.1.call-update) | async-done | bytes 1048592 | tf_op jit(solution)/shard_map/all_gather | solution.py:117
  32.9 32.9 %shard_map.64 = f32[32,6144]{1,0:T(8,128)} custom-call(bf16[4,64,2048]{2,1,0:T(8,128)(2,1)} %all-gather.2.cloned.1.call-done.pairs_ref, bf16[4,64,6144]{2,1,0:T(8,128)(2,1)} %val_ref.3, bf16[4,64,6144]{2,1,0:T(8,128)(2,1)} %cond_ref.3), custom_call_target="tpu_custom_call" | custom-call | tf_op jit(solution)/shard_map/pallas_call | solution.py:48
  65.8 0.0 reduce-scatter.3.cloned.1.call-update
  65.9 0.0 reduce-scatter.5.cloned.1.call-start
  65.9 56.8 %reduce-scatter.3.cloned.1.call-done = f32[32,384]{1,0:T(8,128)} async-done(((f32[32,6144]{1,0:T(8,128)}), f32[32,384]{1,0:T(8,128)}) %reduce-scatter.3.cloned.1.call-update) | async-done | bytes 49168 | tf_op jit(solution)/shard_map/reduce_scatter | solution.py:119
  122.8 0.8 convert_element_type.14
  123.6 20.5 %all_gather.10 = bf16[32,6144]{1,0:T(8,128)(2,1)S(1)} all-gather(bf16[32,384]{1,0:T(8,128)(2,1)S(1)} %convert_element_type.14), channel_id=1, replica_groups=mesh['ka'=16,'pa'=2] {'ka'}, dimensions={1}, use_global_device_ids=true | all-gather | bytes 417792 | tf_op jit(solution)/shard_map/all_gather | solution.py:120
  144.0 0.0 copy-start.1
  144.0 6.6 %convolution_convert_fusion = bf16[32,768]{1,0:T(8,128)(2,1)S(1)} fusion(bf16[32,6144]{1,0:T(8,128)(2,1)S(1)} %all_gather.10, bf16[768,6144]{1,0:T(8,128)(2,1)} %param.11), kind=kOutput, calls=%fused_computation | convolution fusion | flops 302014464 | bytes 9879552 | tf_op jit(solution)/shard_map/dot_general | solution.py:121
  150.6 8.6 %psum.7 = bf16[32,768]{1,0:T(8,128)(2,1)S(1)} all-reduce(bf16[32,768]{1,0:T(8,128)(2,1)S(1)} %convolution_convert_fusion), channel_id=1, replica_groups=mesh['ka'=16,'pa'=2] {'pa'}, use_global_device_ids=true, to_apply=%region_1.0 | all-reduce | flops 24576 | bytes 98304 | tf_op jit(solution)/shard_map/psum | solution.py:124
  159.2 19.6 %all_gather.11 = bf16[32,12288]{1,0:T(8,128)(2,1)S(1)} all-gather(bf16[32,768]{1,0:T(8,128)(2,1)S(1)} %psum.7), channel_id=1, replica_groups=mesh['ka'=16,'pa'=2] {'ka'}, dimensions={1}, use_global_device_ids=true | all-gather | bytes 835584 | tf_op jit(solution)/shard_map/all_gather | solution.py:125
  178.8 0.8 constant_dynamic-slice_fusion.image_ref
  179.6 36.1 %shard_map.65 = bf16[4,64,2048]{2,1,0:T(8,128)(2,1)} custom-call(bf16[32,6144]{1,0:T(8,128)(2,1)} %constant_dynamic-slice_fusion.image_ref, bf16[4,64,6144]{2,1,0:T(8,128)(2,1)} %val_ref.3, bf16[4,64,6144]{2,1,0:T(8,128)(2,1)} %cond_ref.3), custom_call_target="tpu_custom_call" | custom-call | tf_op jit(solution)/shard_map/pallas_call | solution.py:96
  215.7 0.0 reduce-scatter.5.cloned.1.call-update
  215.8 0.0 copy-done
  215.8 0.1 dynamic-slice_bitcast_fusion
  215.8 0.0 copy-done.1
  215.8 0.1 broadcast_subtract_fusion
  215.9 0.1 mul.18
  216.1 0.7 mul.19
  216.7 17.1 %reduce-scatter.5.cloned.1.call-done = bf16[4,32,2048]{2,1,0:T(8,128)(2,1)} async-done(((bf16[4,64,2048]{2,1,0:T(8,128)(2,1)}), bf16[4,32,2048]{2,1,0:T(8,128)(2,1)}) %reduce-scatter.5.cloned.1.call-update) | async-done | bytes 524304 | tf_op jit(solution)/shard_map/reduce_scatter | solution.py:130
  233.9 1.6 fusion
  235.5 1.2 copy.9
Async XLA Ops:
  6.5 209.2 %copy-start = (f32[4,64]{1,0:T(4,128)S(1)}, f32[4,64]{1,0:T(4,128)}, u32[]{:S(2)}) copy-start(f32[4,64]{1,0:T(4,128)} %param.7) | copy-start | bytes 3076
  6.5 26.4 %all-gather.2.cloned.1.call-start = ((), (), s32[]{:S(2)}) async-start(), calls=%async_computation.2 | async-start | bytes 1572864 | tf_op jit(solution)/shard_map/all_gather | solution.py:117
  8.7 114.1 %reduce-scatter.3.cloned.1.call-start = ((), (), s32[]{:S(2)}) async-start(), calls=%async_computation.3 | async-start | bytes 835584 | tf_op jit(solution)/shard_map/reduce_scatter | solution.py:119
  65.9 168.0 %reduce-scatter.5.cloned.1.call-start = ((), (), s32[]{:S(2)}) async-start(), calls=%async_computation.4 | async-start | bytes 1572864 | tf_op jit(solution)/shard_map/reduce_scatter | solution.py:130
  144.0 71.8 %copy-start.1 = (f32[4,64]{1,0:T(4,128)S(1)}, f32[4,64]{1,0:T(4,128)}, u32[]{:S(2)}) copy-start(f32[4,64]{1,0:T(4,128)} %param.8) | copy-start | bytes 3076
Sparse Core Ops, SparseCore 0:
  8.9 23.9 all-gather.1
  66.0 56.7 reduce-scatter.2
  215.9 17.9 reduce-scatter.4

commit v2 on v1

--- a/solution.py
+++ b/solution.py
@@ -108,7 +108,7 @@
     )(image, orb_val, orb_cond)
 
 
-def body(pairs, eps_val, eps_cond, orb_val, orb_cond, screened):
+def body_plain(pairs, eps_val, eps_cond, orb_val, orb_cond, screened):
     val_rows, kpoints, width = pairs.shape
     conds = orb_cond.shape[1]
     points_dev = orb_val.shape[2]
@@ -136,6 +136,412 @@
     return (diagonal_part + coupling).astype(jnp.bfloat16)
 
 
+MESH = pl.DeviceIdType.MESH
+QUARTER = 8
+
+
+def forward_pair_kernel(vectors, own_ref, val_ref, cond_ref, out_ref, full, turned, early, local_sem, send_sem, recv_sem):
+    kpoints, conds, tile = cond_ref.shape
+    row, me = lax.axis_index("ka"), lax.axis_index("pa")
+    other = 1 - me
+    phase, step = pl.program_id(0), pl.program_id(1)
+
+    def remote(k):
+        return pltpu.make_async_remote_copy(
+            src_ref=own_ref.at[k],
+            dst_ref=full.at[me, k],
+            send_sem=send_sem.at[k],
+            recv_sem=recv_sem.at[k],
+            device_id=(row, other),
+            device_id_type=MESH,
+        )
+
+    def turn(k):
+        remote(k).wait()
+        turned[k] = jnp.concatenate([full[0, k], full[1, k]], axis=0).T
+
+    @pl.when(jnp.logical_and(phase == 0, step == 0))
+    def _():
+        local = pltpu.make_async_copy(own_ref, full.at[me], local_sem)
+        local.start()
+        barrier = pltpu.get_barrier_semaphore()
+        pl.semaphore_signal(barrier, inc=1, device_id=(row, other), device_id_type=MESH)
+        pl.semaphore_wait(barrier, 1)
+        for k in range(kpoints):
+            remote(k).start()
+        local.wait()
+        turn(0)
+
+    @pl.when(jnp.logical_and(phase == 1, step == 0))
+    def _():
+        for k in range(1, kpoints):
+            turn(k)
+
+    group = 4
+
+    def contract(ks, g):
+        total = None
+        for k in ks:
+            wide = cond_ref[k].astype(jnp.float32).reshape(conds // 8, 8, tile)
+            rows = turned[k, g * group * conds : (g + 1) * group * conds, :]
+            inner = jnp.dot(rows, val_ref[k], preferred_element_type=jnp.float32)
+            inner = inner.reshape(group, conds // 8, 8, tile)
+            added = jnp.sum(inner * wide[None], axis=1)
+            total = added if total is None else total + added
+        return jnp.sum(total, axis=1)
+
+    @pl.when(phase == 0)
+    def _():
+        for g in range(vectors // group):
+            early[step, g * group : (g + 1) * group, :] = contract([0], g)
+
+    @pl.when(phase == 1)
+    def _():
+        parts = [contract(range(1, kpoints), g) for g in range(vectors // group)]
+        out_ref[...] = (jnp.concatenate(parts, axis=0) + early[step]).astype(out_ref.dtype)
+
+
+def forward_pair(own, orb_val, orb_cond):
+    kpoints, all_val, points_dev = orb_val.shape
+    conds = orb_cond.shape[1]
+    val_rows, width = own.shape[1:]
+    vectors = width // conds
+    tile = 256
+    return pl.pallas_call(
+        functools.partial(forward_pair_kernel, vectors),
+        grid=(2, points_dev // tile),
+        out_shape=jax.ShapeDtypeStruct((vectors, points_dev), jnp.bfloat16),
+        in_specs=[
+            pl.BlockSpec(memory_space=pl.ANY),
+            pl.BlockSpec((kpoints, all_val, tile), lambda h, i: (0, 0, i)),
+            pl.BlockSpec((kpoints, conds, tile), lambda h, i: (0, 0, i)),
+        ],
+        out_specs=pl.BlockSpec((vectors, tile), lambda h, i: (0, h * i)),
+        scratch_shapes=[
+            pltpu.VMEM((2, kpoints, val_rows, width), jnp.bfloat16),
+            pltpu.VMEM((kpoints, width, all_val), jnp.bfloat16),
+            pltpu.VMEM((points_dev // tile, vectors, tile), jnp.float32),
+            pltpu.SemaphoreType.DMA,
+            pltpu.SemaphoreType.DMA((kpoints,)),
+            pltpu.SemaphoreType.DMA((kpoints,)),
+        ],
+        compiler_params=pltpu.CompilerParams(
+            vmem_limit_bytes=VMEM_BYTES, collective_id=0, has_side_effects=True
+        ),
+    )(own, orb_val, orb_cond)
+
+
+def middle_kernel(
+    count, part_ref, screened_ref, out_ref, near, landed, points, piece, summed, images,
+    near_sem, sum_send, sum_recv, pts_send, pts_recv, mix_send, mix_recv, img_send, img_recv,
+):
+    me, plane = lax.axis_index("ka"), lax.axis_index("pa")
+    share = landed.shape[2]
+    rows_dev = near.shape[0]
+    vectors = points.shape[0]
+    quarters = vectors // QUARTER
+    ring = count // quarters
+    layers = quarters // 2
+
+    def cols(j, size):
+        return pl.ds(pl.multiple_of(j * size, 128), size)
+
+    load = pltpu.make_async_copy(screened_ref, near, near_sem)
+    load.start()
+
+    barrier = pltpu.get_barrier_semaphore()
+    for s in range(1, 2 * count):
+        there = lax.rem(me * 2 + plane + s, 2 * count)
+        pl.semaphore_signal(
+            barrier, inc=1, device_id=(there // 2, lax.rem(there, 2)), device_id_type=MESH
+        )
+    pl.semaphore_wait(barrier, 2 * count - 1)
+
+    def send_part(j, slot):
+        return pltpu.make_async_remote_copy(
+            src_ref=part_ref.at[:, cols(j, share)],
+            dst_ref=landed.at[slot],
+            send_sem=sum_send.at[j],
+            recv_sem=sum_recv.at[slot],
+            device_id=(j, plane),
+            device_id_type=MESH,
+        )
+
+    def send_points(j, owner):
+        return pltpu.make_async_remote_copy(
+            src_ref=points.at[:, cols(owner, share)],
+            dst_ref=points.at[:, cols(owner, share)],
+            send_sem=pts_send.at[j],
+            recv_sem=pts_recv.at[owner],
+            device_id=(j, plane),
+            device_id_type=MESH,
+        )
+
+    def send_images(j, owner):
+        return pltpu.make_async_remote_copy(
+            src_ref=images.at[owner],
+            dst_ref=images.at[owner],
+            send_sem=img_send.at[j],
+            recv_sem=img_recv.at[owner],
+            device_id=(j, plane),
+            device_id_type=MESH,
+        )
+
+    ahead = [lax.rem(me + s, count) for s in range(1, count)]
+    behind = [lax.rem(me + count - s, count) for s in range(1, count)]
+
+    for j in ahead:
+        send_part(j, me).start()
+    total = part_ref[:, cols(me, share)].astype(jnp.float32)
+    for j in behind:
+        send_part(j, j).wait_recv()
+        total = total + landed[j].astype(jnp.float32)
+    points[:, cols(me, share)] = total.astype(jnp.bfloat16)
+    for j in ahead:
+        send_points(j, me).start()
+
+    load.wait()
+    image = None
+    for s in range(count // 2):
+        t = lax.rem(me // 2 + count // 2 - s, count // 2)
+        if s == 0:
+            send_points(t * 2 + 1 - lax.rem(me, 2), t * 2 + 1 - lax.rem(me, 2)).wait_recv()
+        else:
+            send_points(t * 2, t * 2).wait_recv()
+            send_points(t * 2 + 1, t * 2 + 1).wait_recv()
+        added = lax.dot_general(
+            points[:, cols(t, 2 * share)],
+            near[:, cols(t, 2 * share)],
+            (((1,), (1,)), ((), ())),
+            preferred_element_type=jnp.float32,
+        )
+        image = added if image is None else image + added
+    for t in range(quarters):
+        piece[t] = image[t * QUARTER : (t + 1) * QUARTER, :]
+
+    z, r = me // ring, lax.rem(me, ring)
+    target, layer = z // layers, lax.rem(z, layers)
+
+    def send_piece(t, source_plane, source_layer):
+        return pltpu.make_async_remote_copy(
+            src_ref=piece.at[t],
+            dst_ref=summed.at[source_plane, source_layer],
+            send_sem=mix_send.at[t],
+            recv_sem=mix_recv.at[source_plane * layers + source_layer],
+            device_id=(t * ring + r, target),
+            device_id_type=MESH,
+        )
+
+    for t in range(quarters):
+        here = jnp.logical_and(target == plane, z == t)
+
+        @pl.when(jnp.logical_not(here))
+        def _():
+            send_piece(t, plane, layer).start()
+
+        @pl.when(here)
+        def _():
+            summed[plane, layer] = piece[t]
+
+    for p in range(2):
+        for h in range(layers):
+            here = jnp.logical_and(p == plane, z == plane * layers + h)
+
+            @pl.when(jnp.logical_not(here))
+            def _():
+                send_piece(0, p, h).wait_recv()
+
+    for h in range(layers):
+        images[me, :, h * rows_dev : (h + 1) * rows_dev] = (summed[0, h] + summed[1, h]).astype(
+            jnp.bfloat16
+        )
+    for j in ahead:
+        send_images(j, me).start()
+    for j in ahead:
+        send_part(j, me).wait_send()
+        send_points(j, me).wait_send()
+    for t in range(quarters):
+        here = jnp.logical_and(target == plane, z == t)
+
+        @pl.when(jnp.logical_not(here))
+        def _():
+            send_piece(t, plane, layer).wait_send()
+
+    for j in behind:
+        send_images(j, j).wait_recv()
+    for f in range(quarters // 2):
+        for c in range(ring):
+            both = jnp.concatenate(
+                [images[(2 * f + e) * ring + c].astype(jnp.float32) for e in range(2)], axis=0
+            ).astype(jnp.bfloat16)
+            for h in range(layers):
+                at = (h * ring + c) * rows_dev
+                out_ref[f * 2 * QUARTER : (f + 1) * 2 * QUARTER, at : at + rows_dev] = both[
+                    :, h * rows_dev : (h + 1) * rows_dev
+                ]
+    for j in ahead:
+        send_images(j, me).wait_send()
+
+
+def middle(count, part, screened):
+    vectors, points_dev = part.shape
+    rows_dev = screened.shape[0]
+    share = points_dev // count
+    layers = vectors // QUARTER // 2
+    dma = pltpu.SemaphoreType.DMA
+    return pl.pallas_call(
+        functools.partial(middle_kernel, count),
+        out_shape=jax.ShapeDtypeStruct((vectors, points_dev), jnp.bfloat16),
+        in_specs=[pl.BlockSpec(memory_space=pltpu.VMEM), pl.BlockSpec(memory_space=pl.ANY)],
+        out_specs=pl.BlockSpec(memory_space=pltpu.VMEM),
+        scratch_shapes=[
+            pltpu.VMEM((rows_dev, points_dev), jnp.bfloat16),
+            pltpu.VMEM((count, vectors, share), jnp.bfloat16),
+            pltpu.VMEM((vectors, points_dev), jnp.bfloat16),
+            pltpu.VMEM((vectors // QUARTER, QUARTER, rows_dev), jnp.float32),
+            pltpu.VMEM((2, layers, QUARTER, rows_dev), jnp.float32),
+            pltpu.VMEM((count, QUARTER, layers * rows_dev), jnp.bfloat16),
+            dma,
+            dma((count,)),
+            dma((count,)),
+            dma((count,)),
+            dma((count,)),
+            dma((vectors // QUARTER,)),
+            dma((2 * layers,)),
+            dma((count,)),
+            dma((count,)),
+        ],
+        compiler_params=pltpu.CompilerParams(
+            vmem_limit_bytes=VMEM_BYTES, collective_id=1, has_side_effects=True
+        ),
+    )(part, screened)
+
+
+def backward_pair_kernel(
+    image_ref, val_ref, cond_ref, own_ref, level_val_ref, level_cond_ref, out_ref,
+    total, kept, away, landed, send_sem, recv_sem,
+):
+    vectors, tile = image_ref.shape
+    conds = cond_ref.shape[1]
+    kpoints, val_rows = own_ref.shape[:2]
+    group = 4
+    at, step = pl.program_id(0), pl.program_id(1)
+    row, me = lax.axis_index("ka"), lax.axis_index("pa")
+    other = 1 - me
+
+    def remote(k):
+        return pltpu.make_async_remote_copy(
+            src_ref=away.at[k],
+            dst_ref=landed.at[k],
+            send_sem=send_sem.at[k],
+            recv_sem=recv_sem.at[k],
+            device_id=(row, other),
+            device_id_type=MESH,
+        )
+
+    @pl.when(jnp.logical_and(at == 0, step == 0))
+    def _():
+        barrier = pltpu.get_barrier_semaphore()
+        pl.semaphore_signal(barrier, inc=1, device_id=(row, other), device_id_type=MESH)
+        pl.semaphore_wait(barrier, 1)
+
+    @pl.when(step == 0)
+    def _():
+        total[...] = jnp.zeros_like(total)
+
+    valence = val_ref[0]
+    conduction = cond_ref[0]
+    for g in range(vectors // group):
+        pieces = [
+            jnp.broadcast_to(image_ref[b : b + 1, :], (conds, tile)) * conduction
+            for b in range(g * group, (g + 1) * group)
+        ]
+        mixed = jnp.concatenate(pieces, axis=0)
+        cols = slice(g * group * conds, (g + 1) * group * conds)
+        total[:, cols] += lax.dot_general(
+            valence, mixed, (((1,), (1,)), ((), ())), preferred_element_type=jnp.float32
+        )
+
+    def finish(k):
+        remote(k).wait()
+        gap = level_cond_ref[k] - level_val_ref[k]
+        coupling = kept[k] + landed[k].astype(jnp.float32)
+        out_ref[k] = (gap * own_ref[k].astype(jnp.float32) + coupling).astype(out_ref.dtype)
+
+    @pl.when(step == pl.num_programs(1) - 1)
+    def _():
+        away[at] = total[pl.ds(pl.multiple_of(other * val_rows, 8), val_rows), :].astype(away.dtype)
+        remote(at).start()
+        kept[at] = total[pl.ds(pl.multiple_of(me * val_rows, 8), val_rows), :]
+
+        @pl.when(at >= 1)
+        def _():
+            finish(at - 1)
+
+        @pl.when(at == kpoints - 1)
+        def _():
+            finish(at)
+
+
+def backward_pair(image, orb_val, orb_cond, own, level_val, level_cond):
+    kpoints, all_val, points_dev = orb_val.shape
+    conds = orb_cond.shape[1]
+    vectors = image.shape[0]
+    val_rows, width = own.shape[1:]
+    tile = pick_tile(points_dev, 1024)
+    fixed = lambda k, i: (0, 0, 0)
+    return pl.pallas_call(
+        backward_pair_kernel,
+        grid=(kpoints, points_dev // tile),
+        out_shape=jax.ShapeDtypeStruct(own.shape, jnp.bfloat16),
+        in_specs=[
+            pl.BlockSpec((vectors, tile), lambda k, i: (0, i)),
+            pl.BlockSpec((1, all_val, tile), lambda k, i: (k, 0, i)),
+            pl.BlockSpec((1, conds, tile), lambda k, i: (k, 0, i)),
+            pl.BlockSpec(own.shape, fixed),
+            pl.BlockSpec(level_val.shape, fixed),
+            pl.BlockSpec(level_cond.shape, fixed),
+        ],
+        out_specs=pl.BlockSpec(own.shape, fixed),
+        scratch_shapes=[
+            pltpu.VMEM((all_val, width), jnp.float32),
+            pltpu.VMEM(own.shape, jnp.float32),
+            pltpu.VMEM(own.shape, jnp.bfloat16),
+            pltpu.VMEM(own.shape, jnp.bfloat16),
+            pltpu.SemaphoreType.DMA((kpoints,)),
+            pltpu.SemaphoreType.DMA((kpoints,)),
+        ],
+        compiler_params=pltpu.CompilerParams(
+            vmem_limit_bytes=VMEM_BYTES, collective_id=2, has_side_effects=True
+        ),
+    )(image, orb_val, orb_cond, own, level_val, level_cond)
+
+
+def body_direct(count, pairs, eps_val, eps_cond, orb_val, orb_cond, screened):
+    val_rows, kpoints, width = pairs.shape
+    conds = orb_cond.shape[1]
+    vectors = width // conds
+    own = jnp.transpose(pairs, (1, 0, 2))
+    own_val = lax.dynamic_slice_in_dim(eps_val, lax.axis_index("pa") * val_rows, val_rows, 1)
+    level_cond = jnp.tile(eps_cond, (1, vectors))[:, None, :]
+    part = forward_pair(own, orb_val, orb_cond)
+    image = middle(count, part, screened)
+    result = backward_pair(image, orb_val, orb_cond, own, own_val[:, :, None], level_cond)
+    return jnp.transpose(result, (1, 0, 2))
+
+
+def body(count, planes, *args):
+    pairs, orb_val, orb_cond, screened = args[0], args[3], args[4], args[5]
+    points_dev, rows_dev = orb_val.shape[2], screened.shape[0]
+    vectors = pairs.shape[2] // orb_cond.shape[1]
+    aligned = points_dev % (128 * count) == 0 and rows_dev % 128 == 0 and points_dev % 256 == 0
+    quarters = vectors // QUARTER
+    even = vectors % (2 * QUARTER) == 0 and count % max(quarters, 1) == 0 and quarters % 2 == 0
+    if planes == 2 and aligned and even and pairs.shape[0] % 16 == 0:
+        return body_direct(count, *args)
+    return body_plain(*args)
+
+
 def solution(mesh):
     in_specs = (
         P("pa", "ka", None),
@@ -146,4 +552,5 @@
         P("ka", "pa"),
     )
     out_specs = P("pa", "ka", None)
-    return jax.shard_map(body, mesh=mesh, in_specs=in_specs, out_specs=out_specs, check_vma=False)
+    step = functools.partial(body, mesh.shape["ka"], mesh.shape["pa"])
+    return jax.shard_map(step, mesh=mesh, in_specs=in_specs, out_specs=out_specs, check_vma=False)

time: 244 us -> 145 us (0.59)
  waiting for transfers between devices: 98.2 us -> 0 us
  Pallas kernels: 69 us -> 136 us
  blocking collectives: 48.7 us -> 0 us
  between operations: 13.2 us -> 0.03 us
  matrix products: 6.59 us -> 0 us
  other arithmetic: 2.49 us -> 0 us
    reduce_scatter x2 -> x0, waiting for transfers between devices: 74 us -> none  [the longest x1 56.8 us: body(): lax.psum_scatter(partial_points, 'ka', scatter_dimension=1, tiled=True)]
    pallas_call x2 -> x3, Pallas kernels: 69 us -> 136 us  [the longest x1 51.9 us: forward_pair(): pl.pallas_call(functools.partial(forward_pair_kernel, vectors), grid=(2,...]
    all_gather x2 -> x0, blocking collectives: 40.1 us -> none  [the longest x1 20.5 us: body(): lax.all_gather(points.astype(jnp.bfloat16), 'ka', axis=1, tiled=True)]
    all_gather x1 -> x0, waiting for transfers between devices: 24.2 us -> none  [body(): rows = lax.all_gather(own, 'pa', axis=1, tiled=True)]
    psum x1 -> x0, blocking collectives: 8.61 us -> none  [body(): image_rows = lax.psum(image_part.astype(jnp.bfloat16), 'pa')]
    dot_general x1 -> x0, matrix products: 6.59 us -> none  [body(): lax.dot_general(points_bf, screened, (((1,), (1,)), ((), ())), preferred_...]
  transfers between devices with their start and end apart: 3 -> 0, of which waited for: 3 -> 0; matrix products, arithmetic and copies ran while one was open for 0% -> 0% of each run, Pallas kernels for 0% -> 0%
where the time goes in v2:
time: 145 us; the launch traced here: 144 us
  Pallas kernels  136 us (94%)
  local copies, waits for them, and re-layouts  7.26 us (5%)
    pallas_call x1, Pallas kernels, forward_pair(): pl.pallas_call(functools.partial(forward_pair_kernel, vectors), grid=(2,...  51.9 us
    pallas_call x1, Pallas kernels, backward_pair(): pl.pallas_call(backward_pair_kernel, grid=(kpoints, points_dev // tile),...  44.4 us
    pallas_call x1, Pallas kernels, middle(): pl.pallas_call(functools.partial(middle_kernel, count), out_shape=jax.Sha...  40.1 us

profile of v2, /device:TPU:0, one launch (start us, length us, event | category | flops | bytes accessed | tf_op | source)
XLA Modules:
  0.0 143.7 jit_solution(12930275822987455757)
XLA Ops:
  0.0 0.0 copy-start
  0.0 0.7 copy-done
  0.7 0.1 dynamic-slice_bitcast_fusion
  0.8 0.7 copy.8.level_val_ref
  1.5 0.7 tile.8
  2.2 0.7 tile.9.level_cond_ref
  2.9 2.1 %copy.11 = bf16[32,4,2048]{2,0,1:T(8,128)(2,1)} copy(bf16[32,4,2048]{2,1,0:T(4,128)(2,1)} %param.6) | data formatting | bytes 1048576 | tf_op args[0]
  5.0 51.9 %shard_map.64.part_ref = bf16[32,6144]{1,0:T(8,128)(2,1)} custom-call(bf16[4,32,2048]{2,1,0:T(8,128)(2,1)} %bitcast.6, bf16[4,64,6144]{2,1,0:T(8,128)(2,1)} %val_ref.3, bf16[4,64,6144]{2,1,0:T(8,128)(2,1)} %cond_ref.3), custom_call_target="tpu_custom_call" | custom-call | tf_op jit(solution)/shard_map/pallas_call | solution.py:210
  56.9 40.1 %shard_map.65.image_ref = bf16[32,6144]{1,0:T(8,128)(2,1)} custom-call(bf16[32,6144]{1,0:T(8,128)(2,1)} %shard_map.64.part_ref, bf16[768,6144]{1,0:T(8,128)(2,1)} %screened_ref.1), custom_call_target="tpu_custom_call" | custom-call | tf_op jit(solution)/shard_map/pallas_call | solution.py:392
  97.0 44.4 %shard_map.66 = bf16[4,32,2048]{2,1,0:T(8,128)(2,1)} custom-call(bf16[32,6144]{1,0:T(8,128)(2,1)} %shard_map.65.image_ref, bf16[4,64,6144]{2,1,0:T(8,128)(2,1)} %val_ref.3, bf16[4,64,6144]{2,1,0:T(8,128)(2,1)} %cond_ref.3, bf16[4,32,2048]{2,1,0:T(8,128)(2,1)} %bitcast.7, f32[4,32,1]{2,1,0:T(8,128)} %copy.8.level_val_ref, f32[4,1,2048]{2,1,0:T(1,128)} %tile.9.level_cond_ref), custom_call_target="tpu_custom_call" | custom-call | tf_op jit(solution)/shard_map/pallas_call | solution.py:493
  141.4 2.2 %copy.9 = bf16[32,4,2048]{2,1,0:T(4,128)(2,1)} copy(bf16[32,4,2048]{2,0,1:T(8,128)(2,1)} %bitcast.8) | data formatting | bytes 1048576 | tf_op jit(solution)/shard_map/transpose | solution.py:530
Async XLA Ops:
  0.0 0.7 copy-start

commit v3 on v2

--- a/solution.py
+++ b/solution.py
@@ -140,114 +140,37 @@
 QUARTER = 8
 
 
-def forward_pair_kernel(vectors, own_ref, val_ref, cond_ref, out_ref, full, turned, early, local_sem, send_sem, recv_sem):
-    kpoints, conds, tile = cond_ref.shape
-    row, me = lax.axis_index("ka"), lax.axis_index("pa")
-    other = 1 - me
-    phase, step = pl.program_id(0), pl.program_id(1)
-
-    def remote(k):
-        return pltpu.make_async_remote_copy(
-            src_ref=own_ref.at[k],
-            dst_ref=full.at[me, k],
-            send_sem=send_sem.at[k],
-            recv_sem=recv_sem.at[k],
-            device_id=(row, other),
-            device_id_type=MESH,
-        )
-
-    def turn(k):
-        remote(k).wait()
-        turned[k] = jnp.concatenate([full[0, k], full[1, k]], axis=0).T
-
-    @pl.when(jnp.logical_and(phase == 0, step == 0))
-    def _():
-        local = pltpu.make_async_copy(own_ref, full.at[me], local_sem)
-        local.start()
-        barrier = pltpu.get_barrier_semaphore()
-        pl.semaphore_signal(barrier, inc=1, device_id=(row, other), device_id_type=MESH)
-        pl.semaphore_wait(barrier, 1)
-        for k in range(kpoints):
-            remote(k).start()
-        local.wait()
-        turn(0)
-
-    @pl.when(jnp.logical_and(phase == 1, step == 0))
-    def _():
-        for k in range(1, kpoints):
-            turn(k)
-
-    group = 4
-
-    def contract(ks, g):
-        total = None
-        for k in ks:
-            wide = cond_ref[k].astype(jnp.float32).reshape(conds // 8, 8, tile)
-            rows = turned[k, g * group * conds : (g + 1) * group * conds, :]
-            inner = jnp.dot(rows, val_ref[k], preferred_element_type=jnp.float32)
-            inner = inner.reshape(group, conds // 8, 8, tile)
-            added = jnp.sum(inner * wide[None], axis=1)
-            total = added if total is None else total + added
-        return jnp.sum(total, axis=1)
-
-    @pl.when(phase == 0)
-    def _():
-        for g in range(vectors // group):
-            early[step, g * group : (g + 1) * group, :] = contract([0], g)
-
-    @pl.when(phase == 1)
-    def _():
-        parts = [contract(range(1, kpoints), g) for g in range(vectors // group)]
-        out_ref[...] = (jnp.concatenate(parts, axis=0) + early[step]).astype(out_ref.dtype)
-
-
-def forward_pair(own, orb_val, orb_cond):
-    kpoints, all_val, points_dev = orb_val.shape
-    conds = orb_cond.shape[1]
-    val_rows, width = own.shape[1:]
-    vectors = width // conds
-    tile = 256
-    return pl.pallas_call(
-        functools.partial(forward_pair_kernel, vectors),
-        grid=(2, points_dev // tile),
-        out_shape=jax.ShapeDtypeStruct((vectors, points_dev), jnp.bfloat16),
-        in_specs=[
-            pl.BlockSpec(memory_space=pl.ANY),
-            pl.BlockSpec((kpoints, all_val, tile), lambda h, i: (0, 0, i)),
-            pl.BlockSpec((kpoints, conds, tile), lambda h, i: (0, 0, i)),
-        ],
-        out_specs=pl.BlockSpec((vectors, tile), lambda h, i: (0, h * i)),
-        scratch_shapes=[
-            pltpu.VMEM((2, kpoints, val_rows, width), jnp.bfloat16),
-            pltpu.VMEM((kpoints, width, all_val), jnp.bfloat16),
-            pltpu.VMEM((points_dev // tile, vectors, tile), jnp.float32),
-            pltpu.SemaphoreType.DMA,
-            pltpu.SemaphoreType.DMA((kpoints,)),
-            pltpu.SemaphoreType.DMA((kpoints,)),
-        ],
-        compiler_params=pltpu.CompilerParams(
-            vmem_limit_bytes=VMEM_BYTES, collective_id=0, has_side_effects=True
-        ),
-    )(own, orb_val, orb_cond)
-
-
-def middle_kernel(
-    count, part_ref, screened_ref, out_ref, near, landed, points, piece, summed, images,
-    near_sem, sum_send, sum_recv, pts_send, pts_recv, mix_send, mix_recv, img_send, img_recv,
+def front_kernel(
+    count, own_ref, val_hbm, cond_hbm, screened_ref, out_ref, val_ref, cond_ref, near, full, turned, early,
+    part_ref, landed, points, piece, summed, images, load_sem, pair_send, pair_recv,
+    sum_send, sum_recv, pts_send, pts_recv, mix_send, mix_recv, img_send, img_recv,
 ):
     me, plane = lax.axis_index("ka"), lax.axis_index("pa")
+    other = 1 - plane
+    core = lax.rem(me, 2)
+    partner = me + 1 - 2 * core
     share = landed.shape[2]
+    kpoints, conds = cond_ref.shape[:2]
     rows_dev = near.shape[0]
-    vectors = points.shape[0]
+    vectors, points_dev = points.shape
+    tile = early.shape[2]
     quarters = vectors // QUARTER
     ring = count // quarters
     layers = quarters // 2
+    chips = count // 2
+    group = 4
 
     def cols(j, size):
         return pl.ds(pl.multiple_of(j * size, 128), size)
 
-    load = pltpu.make_async_copy(screened_ref, near, near_sem)
-    load.start()
+    loads = [
+        pltpu.make_async_copy(own_ref, full.at[plane], load_sem.at[0]),
+        pltpu.make_async_copy(val_hbm, val_ref, load_sem.at[1]),
+        pltpu.make_async_copy(cond_hbm, cond_ref, load_sem.at[2]),
+        pltpu.make_async_copy(screened_ref, near, load_sem.at[3]),
+    ]
+    for load in loads:
+        load.start()
 
     barrier = pltpu.get_barrier_semaphore()
     for s in range(1, 2 * count):
@@ -256,6 +179,16 @@
             barrier, inc=1, device_id=(there // 2, lax.rem(there, 2)), device_id_type=MESH
         )
     pl.semaphore_wait(barrier, 2 * count - 1)
+
+    def send_pairs(k):
+        return pltpu.make_async_remote_copy(
+            src_ref=own_ref.at[k],
+            dst_ref=full.at[plane, k],
+            send_sem=pair_send.at[k],
+            recv_sem=pair_recv.at[k],
+            device_id=(me, other),
+            device_id_type=MESH,
+        )
 
     def send_part(j, slot):
         return pltpu.make_async_remote_copy(
@@ -267,48 +200,104 @@
             device_id_type=MESH,
         )
 
-    def send_points(j, owner):
+    def send_points(j, owner, slot):
         return pltpu.make_async_remote_copy(
             src_ref=points.at[:, cols(owner, share)],
             dst_ref=points.at[:, cols(owner, share)],
-            send_sem=pts_send.at[j],
+            send_sem=pts_send.at[slot],
             recv_sem=pts_recv.at[owner],
             device_id=(j, plane),
             device_id_type=MESH,
         )
 
-    def send_images(j, owner):
+    def send_images(j, owner, slot):
         return pltpu.make_async_remote_copy(
             src_ref=images.at[owner],
             dst_ref=images.at[owner],
-            send_sem=img_send.at[j],
+            send_sem=img_send.at[slot],
             recv_sem=img_recv.at[owner],
             device_id=(j, plane),
             device_id_type=MESH,
         )
 
+    def turn(k):
+        send_pairs(k).wait()
+        turned[k] = jnp.concatenate([full[0, k], full[1, k]], axis=0).T
+
+    def contract(ks, g, at):
+        total = None
+        for k in ks:
+            wide = cond_ref[k, :, at].astype(jnp.float32).reshape(conds // 8, 8, tile)
+            rows = turned[k, g * group * conds : (g + 1) * group * conds, :]
+            inner = jnp.dot(rows, val_ref[k, :, at], preferred_element_type=jnp.float32)
+            inner = inner.reshape(group, conds // 8, 8, tile)
+            added = jnp.sum(inner * wide[None], axis=1)
+            total = added if total is None else total + added
+        return jnp.sum(total, axis=1)
+
+    for k in range(kpoints):
+        send_pairs(k).start()
+    for load in loads[:3]:
+        load.wait()
+    turn(0)
+
+    def first(i, carry):
+        for g in range(vectors // group):
+            early[i, g * group : (g + 1) * group, :] = contract([0], g, cols(i, tile))
+        return carry
+
+    lax.fori_loop(0, points_dev // tile, first, 0)
+    for k in range(1, kpoints):
+        turn(k)
+
+    pieces = 2 * share // tile
+
+    def rest(s, carry):
+        t = lax.rem(me // 2 + 1 + s, chips)
+
+        def inner_tile(u, carry):
+            i = t * pieces + u
+            parts = [contract(range(1, kpoints), g, cols(i, tile)) for g in range(vectors // group)]
+            part_ref[:, cols(i, tile)] = (jnp.concatenate(parts, axis=0) + early[i]).astype(
+                jnp.bfloat16
+            )
+            return carry
+
+        lax.fori_loop(0, pieces, inner_tile, 0)
+        for e in range(2):
+            j = t * 2 + e
+
+            @pl.when(j != me)
+            def _():
+                send_part(j, me).start()
+
+        return carry
+
+    lax.fori_loop(0, chips, rest, 0)
+
     ahead = [lax.rem(me + s, count) for s in range(1, count)]
     behind = [lax.rem(me + count - s, count) for s in range(1, count)]
-
-    for j in ahead:
-        send_part(j, me).start()
+    same_ahead = [lax.rem(me + 2 * s, count) for s in range(1, chips)]
+    same_behind = [lax.rem(me + count - 2 * s, count) for s in range(1, chips)]
+    beside = [lax.rem(partner + count - 2 * s, count) for s in range(chips)]
+
     total = part_ref[:, cols(me, share)].astype(jnp.float32)
     for j in behind:
         send_part(j, j).wait_recv()
         total = total + landed[j].astype(jnp.float32)
     points[:, cols(me, share)] = total.astype(jnp.bfloat16)
-    for j in ahead:
-        send_points(j, me).start()
-
-    load.wait()
+    for j in same_ahead:
+        send_points(j, me, j).start()
+    send_points(partner, me, partner).start()
+    for s, j in enumerate(same_behind):
+        send_points(j, j, j).wait_recv()
+        send_points(partner, j, count + s).start()
+
+    loads[3].wait()
     image = None
-    for s in range(count // 2):
-        t = lax.rem(me // 2 + count // 2 - s, count // 2)
-        if s == 0:
-            send_points(t * 2 + 1 - lax.rem(me, 2), t * 2 + 1 - lax.rem(me, 2)).wait_recv()
-        else:
-            send_points(t * 2, t * 2).wait_recv()
-            send_points(t * 2 + 1, t * 2 + 1).wait_recv()
+    for j in beside:
+        t = j // 2
+        send_points(partner, j, partner).wait_recv()
         added = lax.dot_general(
             points[:, cols(t, 2 * share)],
             near[:, cols(t, 2 * share)],
@@ -355,11 +344,19 @@
         images[me, :, h * rows_dev : (h + 1) * rows_dev] = (summed[0, h] + summed[1, h]).astype(
             jnp.bfloat16
         )
-    for j in ahead:
-        send_images(j, me).start()
+    for j in same_ahead:
+        send_images(j, me, j).start()
+    send_images(partner, me, partner).start()
+    for s, j in enumerate(same_behind):
+        send_images(j, j, j).wait_recv()
+        send_images(partner, j, count + s).start()
     for j in ahead:
         send_part(j, me).wait_send()
-        send_points(j, me).wait_send()
+    for j in same_ahead:
+        send_points(j, me, j).wait_send()
+    send_points(partner, me, partner).wait_send()
+    for s, j in enumerate(same_behind):
+        send_points(partner, j, count + s).wait_send()
     for t in range(quarters):
         here = jnp.logical_and(target == plane, z == t)
 
@@ -367,8 +364,8 @@
         def _():
             send_piece(t, plane, layer).wait_send()
 
-    for j in behind:
-        send_images(j, j).wait_recv()
+    for j in beside:
+        send_images(partner, j, partner).wait_recv()
     for f in range(quarters // 2):
         for c in range(ring):
             both = jnp.concatenate(
@@ -379,42 +376,57 @@
                 out_ref[f * 2 * QUARTER : (f + 1) * 2 * QUARTER, at : at + rows_dev] = both[
                     :, h * rows_dev : (h + 1) * rows_dev
                 ]
-    for j in ahead:
-        send_images(j, me).wait_send()
-
-
-def middle(count, part, screened):
-    vectors, points_dev = part.shape
+    for j in same_ahead:
+        send_images(j, me, j).wait_send()
+    send_images(partner, me, partner).wait_send()
+    for s, j in enumerate(same_behind):
+        send_images(partner, j, count + s).wait_send()
+
+
+def front(count, own, orb_val, orb_cond, screened):
+    kpoints, all_val, points_dev = orb_val.shape
+    conds = orb_cond.shape[1]
+    val_rows, width = own.shape[1:]
+    vectors = width // conds
     rows_dev = screened.shape[0]
     share = points_dev // count
-    layers = vectors // QUARTER // 2
+    tile = 256
+    quarters = vectors // QUARTER
     dma = pltpu.SemaphoreType.DMA
     return pl.pallas_call(
-        functools.partial(middle_kernel, count),
+        functools.partial(front_kernel, count),
         out_shape=jax.ShapeDtypeStruct((vectors, points_dev), jnp.bfloat16),
-        in_specs=[pl.BlockSpec(memory_space=pltpu.VMEM), pl.BlockSpec(memory_space=pl.ANY)],
+        in_specs=[pl.BlockSpec(memory_space=pl.ANY)] * 4,
         out_specs=pl.BlockSpec(memory_space=pltpu.VMEM),
         scratch_shapes=[
+            pltpu.VMEM(orb_val.shape, jnp.bfloat16),
+            pltpu.VMEM(orb_cond.shape, jnp.bfloat16),
             pltpu.VMEM((rows_dev, points_dev), jnp.bfloat16),
+            pltpu.VMEM((2, kpoints, val_rows, width), jnp.bfloat16),
+            pltpu.VMEM((kpoints, width, all_val), jnp.bfloat16),
+            pltpu.VMEM((points_dev // tile, vectors, tile), jnp.float32),
+            pltpu.VMEM((vectors, points_dev), jnp.bfloat16),
             pltpu.VMEM((count, vectors, share), jnp.bfloat16),
             pltpu.VMEM((vectors, points_dev), jnp.bfloat16),
-            pltpu.VMEM((vectors // QUARTER, QUARTER, rows_dev), jnp.float32),
-            pltpu.VMEM((2, layers, QUARTER, rows_dev), jnp.float32),
-            pltpu.VMEM((count, QUARTER, layers * rows_dev), jnp.bfloat16),
-            dma,
+            pltpu.VMEM((quarters, QUARTER, rows_dev), jnp.float32),
+            pltpu.VMEM((2, quarters // 2, QUARTER, rows_dev), jnp.float32),
+            pltpu.VMEM((count, QUARTER, quarters // 2 * rows_dev), jnp.bfloat16),
+            dma((4,)),
+            dma((kpoints,)),
+            dma((kpoints,)),
             dma((count,)),
             dma((count,)),
+            dma((2 * count,)),
             dma((count,)),
-            dma((count,)),
-            dma((vectors // QUARTER,)),
-            dma((2 * layers,)),
-            dma((count,)),
+            dma((quarters,)),
+            dma((quarters,)),
+            dma((2 * count,)),
             dma((count,)),
         ],
         compiler_params=pltpu.CompilerParams(
-            vmem_limit_bytes=VMEM_BYTES, collective_id=1, has_side_effects=True
+            vmem_limit_bytes=VMEM_BYTES, collective_id=0, has_side_effects=True
         ),
-    )(part, screened)
+    )(own, orb_val, orb_cond, screened)
 
 
 def backward_pair_kernel(
@@ -488,7 +500,7 @@
     conds = orb_cond.shape[1]
     vectors = image.shape[0]
     val_rows, width = own.shape[1:]
-    tile = pick_tile(points_dev, 1024)
+    tile = pick_tile(points_dev, 2048)
     fixed = lambda k, i: (0, 0, 0)
     return pl.pallas_call(
         backward_pair_kernel,
@@ -512,7 +524,7 @@
             pltpu.SemaphoreType.DMA((kpoints,)),
         ],
         compiler_params=pltpu.CompilerParams(
-            vmem_limit_bytes=VMEM_BYTES, collective_id=2, has_side_effects=True
+            vmem_limit_bytes=VMEM_BYTES, collective_id=1, has_side_effects=True
         ),
     )(image, orb_val, orb_cond, own, level_val, level_cond)
 
@@ -524,8 +536,7 @@
     own = jnp.transpose(pairs, (1, 0, 2))
     own_val = lax.dynamic_slice_in_dim(eps_val, lax.axis_index("pa") * val_rows, val_rows, 1)
     level_cond = jnp.tile(eps_cond, (1, vectors))[:, None, :]
-    part = forward_pair(own, orb_val, orb_cond)
-    image = middle(count, part, screened)
+    image = front(count, own, orb_val, orb_cond, screened)
     result = backward_pair(image, orb_val, orb_cond, own, own_val[:, :, None], level_cond)
     return jnp.transpose(result, (1, 0, 2))
 
@@ -534,7 +545,7 @@
     pairs, orb_val, orb_cond, screened = args[0], args[3], args[4], args[5]
     points_dev, rows_dev = orb_val.shape[2], screened.shape[0]
     vectors = pairs.shape[2] // orb_cond.shape[1]
-    aligned = points_dev % (128 * count) == 0 and rows_dev % 128 == 0 and points_dev % 256 == 0
+    aligned = points_dev % (128 * count) == 0 and rows_dev % 128 == 0 and points_dev % (256 * count // 2) == 0
     quarters = vectors // QUARTER
     even = vectors % (2 * QUARTER) == 0 and count % max(quarters, 1) == 0 and quarters % 2 == 0
     if planes == 2 and aligned and even and pairs.shape[0] % 16 == 0:

time: 145 us -> 119 us (0.82)
  Pallas kernels: 136 us -> 111 us
    pallas_call x2 -> x1, Pallas kernels: 92 us -> 70.1 us  [front(): pl.pallas_call(functools.partial(front_kernel, count), out_shape=jax.Shap...]
    pallas_call x1, Pallas kernels: 44.4 us -> 41.3 us  [backward_pair(): pl.pallas_call(backward_pair_kernel, grid=(kpoints, points_dev // tile),...]
where the time goes in v3:
time: 119 us
  Pallas kernels  111 us (93%)
  local copies, waits for them, and re-layouts  7.26 us (6%)
    pallas_call x1, Pallas kernels, front(): pl.pallas_call(functools.partial(front_kernel, count), out_shape=jax.Shap...  70.1 us
    pallas_call x1, Pallas kernels, backward_pair(): pl.pallas_call(backward_pair_kernel, grid=(kpoints, points_dev // tile),...  41.3 us
    unnamed x3, local copies, waits for them, and re-layouts  2.81 us

profile of v3, /device:TPU:0, one launch (start us, length us, event | category | flops | bytes accessed | tf_op | source)
XLA Modules:
  0.0 118.6 jit_solution(15915377542986855656)
XLA Ops:
  0.0 0.0 copy-start
  0.0 0.7 copy-done
  0.7 0.1 dynamic-slice_bitcast_fusion
  0.8 0.7 copy.8.level_val_ref
  1.5 0.7 tile.8
  2.2 0.7 tile.9.level_cond_ref
  2.9 2.1 %copy.11 = bf16[32,4,2048]{2,0,1:T(8,128)(2,1)} copy(bf16[32,4,2048]{2,1,0:T(4,128)(2,1)} %param.6) | data formatting | bytes 1048576 | tf_op args[0]
  5.0 70.1 %shard_map.64.image_ref = bf16[32,6144]{1,0:T(8,128)(2,1)} custom-call(bf16[4,32,2048]{2,1,0:T(8,128)(2,1)} %bitcast.6, bf16[4,64,6144]{2,1,0:T(8,128)(2,1)} %val_ref.1, bf16[4,64,6144]{2,1,0:T(8,128)(2,1)} %cond_ref.1, bf16[768,6144]{1,0:T(8,128)(2,1)} %screened_ref.1), custom_call_target="tpu_custom_call" | custom-call | tf_op jit(solution)/shard_map/pallas_call | solution.py:396
  75.1 41.3 %shard_map.65 = bf16[4,32,2048]{2,1,0:T(8,128)(2,1)} custom-call(bf16[32,6144]{1,0:T(8,128)(2,1)} %shard_map.64.image_ref, bf16[4,64,6144]{2,1,0:T(8,128)(2,1)} %val_ref.1, bf16[4,64,6144]{2,1,0:T(8,128)(2,1)} %cond_ref.1, bf16[4,32,2048]{2,1,0:T(8,128)(2,1)} %bitcast.7, f32[4,32,1]{2,1,0:T(8,128)} %copy.8.level_val_ref, f32[4,1,2048]{2,1,0:T(1,128)} %tile.9.level_cond_ref), custom_call_target="tpu_custom_call" | custom-call | tf_op jit(solution)/shard_map/pallas_call | solution.py:505
  116.3 2.2 %copy.9 = bf16[32,4,2048]{2,1,0:T(4,128)(2,1)} copy(bf16[32,4,2048]{2,0,1:T(8,128)(2,1)} %bitcast.8) | data formatting | bytes 1048576 | tf_op jit(solution)/shard_map/transpose | solution.py:541
Async XLA Ops:
  0.0 0.7 copy-start

commit v4 on v3

--- a/solution.py
+++ b/solution.py
@@ -431,7 +431,7 @@
 
 def backward_pair_kernel(
     image_ref, val_ref, cond_ref, own_ref, level_val_ref, level_cond_ref, out_ref,
-    total, kept, away, landed, send_sem, recv_sem,
+    total, streamed, kept, away, landed, send_sem, recv_sem,
 ):
     vectors, tile = image_ref.shape
     conds = cond_ref.shape[1]
@@ -460,18 +460,32 @@
     @pl.when(step == 0)
     def _():
         total[...] = jnp.zeros_like(total)
+        streamed[...] = jnp.zeros_like(streamed)
 
     valence = val_ref[0]
     conduction = cond_ref[0]
-    for g in range(vectors // group):
+    half = vectors // 2
+
+    def products(start, stop):
         pieces = [
             jnp.broadcast_to(image_ref[b : b + 1, :], (conds, tile)) * conduction
-            for b in range(g * group, (g + 1) * group)
+            for b in range(start, stop)
         ]
-        mixed = jnp.concatenate(pieces, axis=0)
+        return jnp.concatenate(pieces, axis=0)
+
+    streamed[...] += lax.dot_general(
+        products(half, vectors),
+        valence,
+        (((1,), (1,)), ((), ())),
+        preferred_element_type=jnp.float32,
+    )
+    for g in range(half // group):
         cols = slice(g * group * conds, (g + 1) * group * conds)
         total[:, cols] += lax.dot_general(
-            valence, mixed, (((1,), (1,)), ((), ())), preferred_element_type=jnp.float32
+            valence,
+            products(g * group, (g + 1) * group),
+            (((1,), (1,)), ((), ())),
+            preferred_element_type=jnp.float32,
         )
 
     def finish(k):
@@ -482,6 +496,7 @@
 
     @pl.when(step == pl.num_programs(1) - 1)
     def _():
+        total[:, half * conds :] = streamed[...].T
         away[at] = total[pl.ds(pl.multiple_of(other * val_rows, 8), val_rows), :].astype(away.dtype)
         remote(at).start()
         kept[at] = total[pl.ds(pl.multiple_of(me * val_rows, 8), val_rows), :]
@@ -500,7 +515,7 @@
     conds = orb_cond.shape[1]
     vectors = image.shape[0]
     val_rows, width = own.shape[1:]
-    tile = pick_tile(points_dev, 2048)
+    tile = pick_tile(points_dev, 1024)
     fixed = lambda k, i: (0, 0, 0)
     return pl.pallas_call(
         backward_pair_kernel,
@@ -517,6 +532,7 @@
         out_specs=pl.BlockSpec(own.shape, fixed),
         scratch_shapes=[
             pltpu.VMEM((all_val, width), jnp.float32),
+            pltpu.VMEM((width // 2, all_val), jnp.float32),
             pltpu.VMEM(own.shape, jnp.float32),
             pltpu.VMEM(own.shape, jnp.bfloat16),
             pltpu.VMEM(own.shape, jnp.bfloat16),

time: 119 us -> 119 us (level)
  no operation moved by 1% of the time
where the time goes in v4:
time: 119 us; the launch traced here: 118 us
  Pallas kernels  111 us (93%)
  local copies, waits for them, and re-layouts  7.26 us (6%)
    pallas_call x1, Pallas kernels, front(): pl.pallas_call(functools.partial(front_kernel, count), out_shape=jax.Shap...  70.1 us
    pallas_call x1, Pallas kernels, backward_pair(): pl.pallas_call(backward_pair_kernel, grid=(kpoints, points_dev // tile),...  41 us
    unnamed x3, local copies, waits for them, and re-layouts  2.81 us

profile of v4, /device:TPU:0, one launch (start us, length us, event | category | flops | bytes accessed | tf_op | source)
XLA Modules:
  0.0 118.3 jit_solution(1694337796419023928)
XLA Ops:
  0.0 0.0 copy-start
  0.0 0.7 copy-done
  0.7 0.1 dynamic-slice_bitcast_fusion
  0.8 0.7 copy.8.level_val_ref
  1.5 0.7 tile.8
  2.2 0.7 tile.9.level_cond_ref
  2.9 2.1 %copy.11 = bf16[32,4,2048]{2,0,1:T(8,128)(2,1)} copy(bf16[32,4,2048]{2,1,0:T(4,128)(2,1)} %param.6) | data formatting | bytes 1048576 | tf_op args[0]
  5.0 70.1 %shard_map.64.image_ref = bf16[32,6144]{1,0:T(8,128)(2,1)} custom-call(bf16[4,32,2048]{2,1,0:T(8,128)(2,1)} %bitcast.6, bf16[4,64,6144]{2,1,0:T(8,128)(2,1)} %val_ref.1, bf16[4,64,6144]{2,1,0:T(8,128)(2,1)} %cond_ref.1, bf16[768,6144]{1,0:T(8,128)(2,1)} %screened_ref.1), custom_call_target="tpu_custom_call" | custom-call | tf_op jit(solution)/shard_map/pallas_call | solution.py:396
  75.1 41.0 %shard_map.65 = bf16[4,32,2048]{2,1,0:T(8,128)(2,1)} custom-call(bf16[32,6144]{1,0:T(8,128)(2,1)} %shard_map.64.image_ref, bf16[4,64,6144]{2,1,0:T(8,128)(2,1)} %val_ref.1, bf16[4,64,6144]{2,1,0:T(8,128)(2,1)} %cond_ref.1, bf16[4,32,2048]{2,1,0:T(8,128)(2,1)} %bitcast.7, f32[4,32,1]{2,1,0:T(8,128)} %copy.8.level_val_ref, f32[4,1,2048]{2,1,0:T(1,128)} %tile.9.level_cond_ref), custom_call_target="tpu_custom_call" | custom-call | tf_op jit(solution)/shard_map/pallas_call | solution.py:520
  116.0 2.2 %copy.9 = bf16[32,4,2048]{2,1,0:T(4,128)(2,1)} copy(bf16[32,4,2048]{2,0,1:T(8,128)(2,1)} %bitcast.8) | data formatting | bytes 1048576 | tf_op jit(solution)/shard_map/transpose | solution.py:557
Async XLA Ops:
  0.0 0.7 copy-start
